TPU v7x, 32 devices: a whole 2x2x4 slice. The times are simulated.
32 devices in a mesh: dp: 16 (over z, y, core), space: 2 (over x).
Axes of the slice: x: 2, y: 2, z: 4, core: 2. Of those that a mesh axis runs over, the one named last changes fastest.
Arguments:
- feature_map: bfloat16 [16, 24, 84, 256], P('dp', 'space'), may hold values from -6 to 6
- proposals: int32 [16, 128, 4], P('dp'), may hold values from 0 to 84, as said below
- hidden_weight: bfloat16 [12544, 512], P(None, 'space'), may hold values from -0.0546875 to 0.0546875
- output_weight: bfloat16 [512, 512], P('space'), may hold values from -0.25 to 0.25
- upstream: bfloat16 [16, 128, 512], P('dp'), may hold values from -6 to 6
Outputs:
- hidden_weight_grad: float32 [12544, 512], P('dp', 'space')
- output_weight_grad: float32 [512, 512], P('space')
- feature_grad: float32 [16, 24, 84, 256], P('dp', 'space')
Inputs may be any that keep to these rules, and one draw needn't show every extreme that they name: `proposals`: each row holds top, left, bottom, right with top < bottom <= 24 and left < right <= 84.
All inputs are finite; a program needn't handle non-finite values.
Results may differ from a plain program's by a relative error of at most 0.012.
Values may be sent and summed in bfloat16 or wider, within the bound.
No kernel may reach another device: no remote copies, remote signals or barrier semaphores. Data moves between devices by JAX's collectives and lax.ppermute only.
A program may use at most 128 MiB of HBM per device.

v0:
```python
import jax
import jax.numpy as jnp
from jax import lax
from jax.sharding import PartitionSpec as P

POOL = 7


def axis_weights(low_edge, high_edge, grid_points):
    edge_start = low_edge.astype(jnp.float32)
    bin_size = (high_edge - low_edge).astype(jnp.float32) / POOL
    bin_index = jnp.arange(POOL).astype(jnp.float32)
    offsets = jnp.array([0.25, 0.75], jnp.float32)
    sample_points = (
        edge_start[:, None, None]
        + (bin_index[None, :, None] + offsets[None, None, :]) * bin_size[:, None, None]
        - 0.5
    )
    weights = jnp.maximum(
        0.0, 1.0 - jnp.abs(sample_points[..., None] - grid_points[None, None, None, :])
    )
    return jnp.mean(weights, axis=2)


def activate(values):
    return jax.nn.gelu(values, approximate=True)


def gelu_grad(values, incoming):
    return jax.vjp(activate, values)[1](incoming)[0]


def block_shape(proposal_count):
    block_size = 32
    return (block_size, proposal_count // block_size)


def crop_rows(own_map, row_weight, col_weight):
    height_cells, width_cells, channels = own_map.shape
    proposal_count = row_weight.shape[0]
    block_size, block_count = block_shape(proposal_count)
    flattened = jnp.transpose(own_map, (1, 0, 2)).reshape(width_cells, height_cells * channels)

    def per_block(blocks):
        row_part, col_part = blocks
        across = jnp.dot(
            col_part.reshape(block_size * POOL, width_cells),
            flattened,
            preferred_element_type=jnp.float32,
        )
        across = across.reshape(block_size, POOL, height_cells, channels)
        return jnp.einsum("riy,rjyc->rijc", row_part, across, precision=lax.Precision.HIGHEST)

    pooled = lax.map(
        per_block,
        (
            row_weight.reshape(block_count, block_size, POOL, height_cells),
            col_weight.reshape(block_count, block_size, POOL, width_cells),
        ),
    )
    return pooled.reshape(proposal_count, POOL * POOL * channels)


def crop_back(grad_pooled, row_weight, col_weight, channels):
    proposal_count, _, height_cells = row_weight.shape
    width_cells = col_weight.shape[2]
    block_size, block_count = block_shape(proposal_count)

    def per_block(running, blocks):
        row_part, col_part, grad_part = blocks
        grad_block = grad_part.reshape(block_size, POOL, POOL, channels)
        spread = jnp.einsum("riy,rijc->rjyc", row_part, grad_block, precision=lax.Precision.HIGHEST)
        added = lax.dot_general(
            col_part.astype(jnp.float32).reshape(block_size * POOL, width_cells),
            spread.reshape(block_size * POOL, height_cells * channels),
            (((0,), (0,)), ((), ())),
            precision=lax.Precision.HIGHEST,
            preferred_element_type=jnp.float32,
        )
        return (running + added, None)

    start = jnp.zeros((width_cells, height_cells * channels), jnp.float32)
    blocks = (
        row_weight.reshape(block_count, block_size, POOL, height_cells),
        col_weight.reshape(block_count, block_size, POOL, width_cells),
        grad_pooled.reshape(block_count, block_size, grad_pooled.shape[1]),
    )
    total, _ = lax.scan(per_block, start, blocks)
    return jnp.transpose(total.reshape(width_cells, height_cells, channels), (1, 0, 2))


def on_device(feature_map, proposals, hidden_weight, output_weight, upstream):
    own_map = feature_map[0]
    corners = proposals[0]
    own_height = own_map.shape[0]
    map_width = own_map.shape[1]
    channels = own_map.shape[2]
    row_offset = lax.axis_index("space") * own_height
    local_grid = (row_offset + jnp.arange(own_height, dtype=jnp.int32)).astype(jnp.float32)
    row_weight = axis_weights(corners[:, 0], corners[:, 2], local_grid)
    col_weight = axis_weights(
        corners[:, 1], corners[:, 3], jnp.arange(map_width, dtype=jnp.int32).astype(jnp.float32)
    ).astype(jnp.bfloat16)
    full_grid = jnp.arange(own_height * lax.axis_size("space"), dtype=jnp.int32).astype(jnp.float32)
    full_weight = axis_weights(corners[:, 0], corners[:, 2], full_grid)
    whole_map = lax.all_gather(own_map, "space", axis=0, tiled=True)
    pooled = crop_rows(whole_map, full_weight, col_weight).astype(jnp.bfloat16)
    pre_hidden = jnp.dot(pooled, hidden_weight, preferred_element_type=jnp.float32)
    hidden = activate(pre_hidden).astype(jnp.bfloat16)
    pre_output = lax.psum(
        jnp.dot(hidden, output_weight, preferred_element_type=jnp.float32).astype(jnp.bfloat16),
        "space",
    ).astype(jnp.float32)
    output_delta = gelu_grad(pre_output, upstream[0].astype(jnp.float32)).astype(jnp.bfloat16)
    step_second = lax.dot_general(
        hidden, output_delta, (((0,), (0,)), ((), ())), preferred_element_type=jnp.float32
    )
    second_total = lax.psum(step_second, "dp")
    hidden_back = lax.dot_general(
        output_delta, output_weight, (((1,), (1,)), ((), ())), preferred_element_type=jnp.float32
    )
    hidden_delta = gelu_grad(pre_hidden, hidden_back).astype(jnp.bfloat16)
    column_rows = lax.all_to_all(pooled, "dp", split_axis=1, concat_axis=0, tiled=True)
    delta_rows = lax.all_gather(hidden_delta, "dp", axis=0, tiled=True)
    first_total = lax.dot_general(
        column_rows, delta_rows, (((0,), (0,)), ((), ())), preferred_element_type=jnp.float32
    )
    partial_grad = lax.dot_general(
        hidden_delta, hidden_weight, (((1,), (1,)), ((), ())), preferred_element_type=jnp.float32
    )
    grad_share = lax.psum_scatter(
        partial_grad.astype(jnp.bfloat16), "space", scatter_dimension=0, tiled=True
    ).astype(jnp.float32)
    pooled_grad = lax.all_gather(
        grad_share.astype(jnp.bfloat16), "space", axis=0, tiled=True
    ).astype(grad_share.dtype)
    map_grad = crop_back(pooled_grad, row_weight, col_weight, channels)
    return (first_total, second_total, map_grad[None])


def solution(mesh):
    placed = (
        P("dp", "space", None, None),
        P("dp", None, None),
        P(None, "space"),
        P("space", None),
        P("dp", None, None),
    )
    return jax.shard_map(
        on_device,
        mesh=mesh,
        in_specs=placed,
        out_specs=(P("dp", "space"), P("space", None), P("dp", "space", None, None)),
        check_vma=False,
    )
```

profile of v0, /device:TPU:0, one launch (start us, length us, event | category | flops | bytes accessed | tf_op | source)
XLA Modules:
  0.0 361.1 jit_solution(6747203176717695255)
XLA Ops:
  9.7 1.0 maximum_reduce_fusion
  11.3 16.2 %all-gather = bf16[1,24,84,256]{3,2,0,1:T(8,128)(2,1)S(1)} all-gather(bf16[1,12,84,256]{3,2,0,1:T(8,128)(2,1)} %bitcast.120), channel_id=2, replica_groups=mesh['dp'=16,'space'=2] {'space'}, dimensions={1}, use_global_device_ids=true | all-gather | bytes 1548288 | tf_op jit(solution)/shard_map/all_gather | solution.py:106
  28.0 34.6 %while.21 = (s32[]{:T(128)}, bf16[4,32,7,7,256]{4,2,3,1,0:T(8,128)(2,1)}, f32[4,32,7,24]{3,2,1,0:T(8,128)S(1)}, bf16[4,32,7,84]{3,1,0,2:T(8,128)(2,1)S(1)}, bf16[84,6144]{1,0:T(8,128)(2,1)S(1)}, /*index=5*/s32[]{:T(128)}) while((s32[]{:T(128)}, bf16[4,32,7,7,256]{4,2,3,1,0:T(8,128)(2,1)}, f32[4,32,7,24]{3,2,1,0:T(8,128)S(1)}, ...), condition=%wide.region_3.4_spmd, body=%wide.region_2.0_spmd.sunk | while | flops 346816512 | bytes 18293832 | solution.py:54
  28.3 0.9 fusion.66
  29.2 7.5 %bitcast_dynamic-update-slice_fusion.2 = bf16[4,32,7,7,256]{4,2,3,1,0:T(8,128)(2,1)} fusion(bf16[4,32,7,7,256]{4,2,3,1,0:T(8,128)(2,1)} %get-tuple-element.230, s32[]{:T(128)} %get-tuple-element.229, f32[32,7,24,256]{3,0,2,1:T(8,128)S(1)} %fusion.66, f32[4,32,7,24]{3,2,1,0:T(8,128)S(1)} %get-tuple-element.237), kind=kOutput, calls=%fused_computation.2.clone.1 | convolution fusion | flops 115605504 | bytes 7472128 | tf_op jit(solution)/shard_map/while/body/eval_jaxpr/riy,rjyc->rijc/dot_general | solution.py:52
  37.0 0.9 fusion.66
  37.8 7.5 %bitcast_dynamic-update-slice_fusion.2 = bf16[4,32,7,7,256]{4,2,3,1,0:T(8,128)(2,1)} fusion(bf16[4,32,7,7,256]{4,2,3,1,0:T(8,128)(2,1)} %get-tuple-element.230, s32[]{:T(128)} %get-tuple-element.229, f32[32,7,24,256]{3,0,2,1:T(8,128)S(1)} %fusion.66, f32[4,32,7,24]{3,2,1,0:T(8,128)S(1)} %get-tuple-element.237), kind=kOutput, calls=%fused_computation.2.clone.1 | convolution fusion | flops 115605504 | bytes 7472128 | tf_op jit(solution)/shard_map/while/body/eval_jaxpr/riy,rjyc->rijc/dot_general | solution.py:52
  46.5 7.5 %bitcast_dynamic-update-slice_fusion.2 = bf16[4,32,7,7,256]{4,2,3,1,0:T(8,128)(2,1)} fusion(bf16[4,32,7,7,256]{4,2,3,1,0:T(8,128)(2,1)} %get-tuple-element.230, s32[]{:T(128)} %get-tuple-element.229, f32[32,7,24,256]{3,0,2,1:T(8,128)S(1)} %fusion.66, f32[4,32,7,24]{3,2,1,0:T(8,128)S(1)} %get-tuple-element.237), kind=kOutput, calls=%fused_computation.2.clone.1 | convolution fusion | flops 115605504 | bytes 7472128 | tf_op jit(solution)/shard_map/while/body/eval_jaxpr/riy,rjyc->rijc/dot_general | solution.py:52
  55.2 7.5 %bitcast_dynamic-update-slice_fusion.2 = bf16[4,32,7,7,256]{4,2,3,1,0:T(8,128)(2,1)} fusion(bf16[4,32,7,7,256]{4,2,3,1,0:T(8,128)(2,1)} %get-tuple-element.230, s32[]{:T(128)} %get-tuple-element.229, f32[32,7,24,256]{3,0,2,1:T(8,128)S(1)} %fusion.66, f32[4,32,7,24]{3,2,1,0:T(8,128)S(1)} %get-tuple-element.237), kind=kOutput, calls=%fused_computation.2.clone.1 | convolution fusion | flops 115605504 | bytes 7472128 | tf_op jit(solution)/shard_map/while/body/eval_jaxpr/riy,rjyc->rijc/dot_general | solution.py:52
  62.6 5.1 %copy.77 = bf16[4,32,7,7,256]{4,3,2,1,0:T(8,128)(2,1)} copy(bf16[4,32,7,7,256]{4,2,3,1,0:T(8,128)(2,1)} %get-tuple-element.57) | data formatting | bytes 6422528 | tf_op jit(solution)/shard_map/convert_element_type | solution.py:107
  67.8 5.6 %convert_element_type.132 = bf16[128,12544]{1,0:T(8,128)(2,1)S(1)} reshape(bf16[4,32,7,7,256]{4,3,2,1,0:T(8,128)(2,1)} %copy.77) | data formatting | bytes 6422528 | tf_op jit(solution)/shard_map/convert_element_type | solution.py:107
  73.4 3.8 %fusion.39 = f32[128,256]{1,0:T(8,128)S(1)} fusion(bf16[128,12544]{1,0:T(8,128)(2,1)S(1)} %convert_element_type.132, bf16[12544,256]{1,0:T(8,128)(2,1)} %param.14), kind=kOutput, calls=%fused_computation.69 | convolution fusion | flops 822083584 | bytes 9764864 | tf_op jit(solution)/shard_map/dot_general | solution.py:108
  79.0 22.9 %all-reduce.3.cloned.1.call-done = bf16[128,512]{1,0:T(8,128)(2,1)} async-done(((bf16[128,512]{1,0:T(8,128)(2,1)}), bf16[128,512]{1,0:T(8,128)(2,1)}) %all-reduce.3.cloned.1.call-update) | async-done | bytes 131088 | tf_op jit(solution)/shard_map/psum | solution.py:110
  101.9 1.2 fusion.24
  103.7 1.1 fusion.37
  104.9 6.8 %convolution_convert_fusion = bf16[128,12544]{1,0:T(8,128)(2,1)} fusion(bf16[128,256]{1,0:T(8,128)(2,1)S(1)} %fusion.37, bf16[12544,256]{1,0:T(8,128)(2,1)} %param.14), kind=kOutput, calls=%fused_computation.21 | convolution fusion | flops 823689216 | bytes 9699328 | tf_op jit(solution)/shard_map/dot_general | solution.py:128
  111.7 9.3 %convert_element_type.129 = bf16[128,16,784]{2,1,0:T(8,128)(2,1)} reshape(bf16[4,32,7,7,256]{4,3,2,1,0:T(8,128)(2,1)} %copy.77) | data formatting | bytes 6422528 | tf_op jit(solution)/shard_map/convert_element_type | solution.py:107
  121.0 6.2 %copy.78 = bf16[128,16,784]{0,2,1:T(8,128)(2,1)} copy(bf16[128,16,784]{2,1,0:T(8,128)(2,1)} %convert_element_type.129) | data formatting | bytes 6422528 | tf_op jit(solution)/shard_map/convert_element_type | solution.py:107
  127.2 5.8 %all-to-all-start = ((bf16[128,16,784]{0,2,1:T(8,128)(2,1)}), bf16[128,16,784]{0,2,1:T(8,128)(2,1)S(1)}, u32[]{:S(2)}, u32[]{:S(2)}) async-start(bf16[128,16,784]{0,2,1:T(8,128)(2,1)} %copy.78), calls=%async_computation | async-start | bytes 6422528 | tf_op jit(solution)/shard_map/all_to_all | solution.py:123
  133.8 22.2 %reduce-scatter.2.cloned.1.call-done = bf16[64,12544]{1,0:T(8,128)(2,1)} async-done(((bf16[128,12544]{1,0:T(8,128)(2,1)}), bf16[64,12544]{1,0:T(8,128)(2,1)}) %reduce-scatter.2.cloned.1.call-update) | async-done | bytes 1605648 | tf_op jit(solution)/shard_map/reduce_scatter | solution.py:131
  156.1 0.9 copy.89
  157.2 1.0 copy.90
  158.2 2.0 fusion.38
  160.2 50.5 %all-gather.4.cloned.1.call-done = bf16[2048,256]{1,0:T(8,128)(2,1)} async-done(((bf16[128,256]{1,0:T(8,128)(2,1)}), bf16[2048,256]{1,0:T(8,128)(2,1)}) %all-gather.4.cloned.1.call-update) | async-done | bytes 1048592 | tf_op jit(solution)/shard_map/all_gather | solution.py:124
  210.8 3.1 fusion.18
  213.9 44.3 %all-gather.6.cloned.1.call-done = bf16[128,12544]{1,0:T(8,128)(2,1)} async-done(((bf16[64,12544]{1,0:T(8,128)(2,1)}), bf16[128,12544]{1,0:T(8,128)(2,1)}) %all-gather.6.cloned.1.call-update) | async-done | bytes 3211280 | tf_op jit(solution)/shard_map/all_gather | solution.py:134
  258.2 5.1 %convert.3 = f32[4,32,12544]{2,1,0:T(8,128)} convert(bf16[4,32,12544]{2,1,0:T(8,128)(2,1)} %bitcast.115) | non-fusion elementwise | flops 1605632 | bytes 9633792 | tf_op jit(solution)/shard_map/reshape | solution.py:86
  263.3 51.9 %while.22 = (s32[]{:T(128)}, f32[84,3072]{1,0:T(8,128)}, bf16[4,32,7,84]{3,2,1,0:T(8,128)(2,1)}, f32[4,32,12544]{2,1,0:T(8,128)}, f32[4,32,7,12]{3,2,1,0:T(8,128)}, /*index=5*/s32[]{:T(128)}, s32[]{:T(128)}) while((s32[]{:T(128)}, f32[84,3072]{1,0:T(8,128)}, bf16[4,32,7,84]{3,2,1,0:T(8,128)(2,1)}, f32[4,32,12544]{2,1,0:T(8,128)}, ...), condition=%wide.region_9.10_spmd.clone, body=%wide.region_8.9_spmd.clone.sunk | while | flops 751951872 | bytes 21422432 | solution.py:88
  263.3 1.5 constant_dynamic-slice_fusion.5
  265.3 4.5 %fusion.71 = f32[32,7,256,12]{2,3,1,0:T(8,128)S(1)} fusion(f32[32,7,7,256]{3,2,1,0:T(8,128)S(1)} %reshape.239, f32[4,32,7,12]{3,2,1,0:T(8,128)} %get-tuple-element.259, s32[]{:T(128)} %get-tuple-element.248), kind=kOutput, calls=%fused_computation.14.clone.1 | convolution fusion | flops 57802752 | bytes 4489728 | tf_op jit(solution)/shard_map/while/body/eval_jaxpr/riy,rijc->rjyc/dot_general | solution.py:72
  269.8 2.4 copy.120
  273.1 2.2 convolution_add_fusion.2
  275.3 1.5 constant_dynamic-slice_fusion.5
  277.3 4.5 %fusion.71 = f32[32,7,256,12]{2,3,1,0:T(8,128)S(1)} fusion(f32[32,7,7,256]{3,2,1,0:T(8,128)S(1)} %reshape.239, f32[4,32,7,12]{3,2,1,0:T(8,128)} %get-tuple-element.259, s32[]{:T(128)} %get-tuple-element.248), kind=kOutput, calls=%fused_computation.14.clone.1 | convolution fusion | flops 57802752 | bytes 4489728 | tf_op jit(solution)/shard_map/while/body/eval_jaxpr/riy,rijc->rjyc/dot_general | solution.py:72
  281.8 2.4 copy.120
  285.1 3.5 convolution_add_fusion.2
  288.6 1.5 constant_dynamic-slice_fusion.5
  290.6 4.5 %fusion.71 = f32[32,7,256,12]{2,3,1,0:T(8,128)S(1)} fusion(f32[32,7,7,256]{3,2,1,0:T(8,128)S(1)} %reshape.239, f32[4,32,7,12]{3,2,1,0:T(8,128)} %get-tuple-element.259, s32[]{:T(128)} %get-tuple-element.248), kind=kOutput, calls=%fused_computation.14.clone.1 | convolution fusion | flops 57802752 | bytes 4489728 | tf_op jit(solution)/shard_map/while/body/eval_jaxpr/riy,rijc->rjyc/dot_general | solution.py:72
  295.1 2.4 copy.120
  298.4 3.5 convolution_add_fusion.2
  301.9 1.5 constant_dynamic-slice_fusion.5
  303.9 4.5 %fusion.71 = f32[32,7,256,12]{2,3,1,0:T(8,128)S(1)} fusion(f32[32,7,7,256]{3,2,1,0:T(8,128)S(1)} %reshape.239, f32[4,32,7,12]{3,2,1,0:T(8,128)} %get-tuple-element.259, s32[]{:T(128)} %get-tuple-element.248), kind=kOutput, calls=%fused_computation.14.clone.1 | convolution fusion | flops 57802752 | bytes 4489728 | tf_op jit(solution)/shard_map/while/body/eval_jaxpr/riy,rijc->rjyc/dot_general | solution.py:72
  308.4 2.4 copy.120
  311.7 3.5 convolution_add_fusion.2
  315.2 1.6 reshape.224
  316.8 2.0 copy.84
  318.8 33.9 %all-reduce.5.cloned.1.call-done = f32[256,512]{1,0:T(8,128)} async-done(((f32[256,512]{1,0:T(8,128)}), f32[256,512]{1,0:T(8,128)}) %all-reduce.5.cloned.1.call-update) | async-done | bytes 524304 | tf_op jit(solution)/shard_map/psum | solution.py:118
  352.7 1.9 copy.136
  (70 shorter events, 15.3 us)
Async XLA Ops:
  7.2 70.7 %copy-start = (bf16[256,512]{1,0:T(8,128)(2,1)S(1)}, bf16[256,512]{1,0:T(8,128)(2,1)}, u32[]{:S(2)}) copy-start(bf16[256,512]{1,0:T(8,128)(2,1)} %param.15) | copy-start | bytes 786436
  7.2 94.7 %all-reduce.3.cloned.1.call-start = ((), (), s32[]{:S(2)}) async-start(), calls=%async_computation.2 | async-start | bytes 262144 | tf_op jit(solution)/shard_map/psum | solution.py:110
  10.7 17.0 %copy-start.2 = (bf16[128,7,84]{0,2,1:T(8,128)(2,1)}, bf16[128,7,84]{0,2,1:T(8,128)(2,1)S(1)}, u32[]{:S(2)}) copy-start(bf16[128,7,84]{0,2,1:T(8,128)(2,1)S(1)} %multiply_convert_fusion) | copy-start | bytes 451588
  77.2 0.7 copy-start.4
  78.7 77.3 %reduce-scatter.2.cloned.1.call-start = ((), (), s32[]{:S(2)}) async-start(), calls=%async_computation.5 | async-start | bytes 4816896 | tf_op jit(solution)/shard_map/reduce_scatter | solution.py:131
  103.0 0.6 copy-start.6
  104.8 6.8 %copy-start.7 = (bf16[128,256]{1,0:T(8,128)(2,1)}, bf16[128,256]{1,0:T(8,128)(2,1)S(1)}, u32[]{:S(2)}) copy-start(bf16[128,256]{1,0:T(8,128)(2,1)S(1)} %fusion.37) | copy-start | bytes 196612
  127.2 28.8 %copy-start.3 = (bf16[128,7,84]{0,2,1:T(8,128)(2,1)S(1)}, bf16[128,7,84]{0,2,1:T(8,128)(2,1)}, u32[]{:S(2)}) copy-start(bf16[128,7,84]{0,2,1:T(8,128)(2,1)} %copy-done.2) | copy-start | bytes 451588
  127.2 31.0 %copy-start.5 = (f32[128,256]{1,0:T(8,128)S(1)}, f32[128,256]{1,0:T(8,128)}, u32[]{:S(2)}) copy-start(f32[128,256]{1,0:T(8,128)} %copy-done.4) | copy-start | bytes 393220
  127.2 83.6 %all-to-all-start = ((bf16[128,16,784]{0,2,1:T(8,128)(2,1)}), bf16[128,16,784]{0,2,1:T(8,128)(2,1)S(1)}, u32[]{:S(2)}, u32[]{:S(2)}) async-start(bf16[128,16,784]{0,2,1:T(8,128)(2,1)} %copy.78), calls=%async_computation | async-start | bytes 6422528 | tf_op jit(solution)/shard_map/all_to_all | solution.py:123
  133.0 77.8 %all-gather.4.cloned.1.call-start = ((), (), s32[]{:S(2)}) async-start(), calls=%async_computation.3 | async-start | bytes 1114112 | tf_op jit(solution)/shard_map/all_gather | solution.py:124
  133.7 124.4 %all-gather.6.cloned.1.call-start = ((), (), s32[]{:S(2)}) async-start(), calls=%async_computation.6 | async-start | bytes 4816896 | tf_op jit(solution)/shard_map/all_gather | solution.py:134
  156.0 196.7 %all-reduce.5.cloned.1.call-start = ((), (), s32[]{:S(2)}) async-start(), calls=%async_computation.4 | async-start | bytes 1048576 | tf_op jit(solution)/shard_map/psum | solution.py:118
  315.2 39.4 %copy-start.1 = (bf16[256,512]{1,0:T(8,128)(2,1)S(1)}, bf16[256,512]{1,0:T(8,128)(2,1)}, u32[]{:S(2)}) copy-start(bf16[256,512]{1,0:T(8,128)(2,1)} %param.15) | copy-start | bytes 786436
Sparse Core Ops, SparseCore 0:
  78.9 22.9 all-reduce.2
  111.8 44.1 reduce-scatter.1
  158.2 52.5 all-gather.3
  212.2 45.9 all-gather.5
  262.0 90.6 all-reduce.4
where the time goes:
time: 363 us; the launch traced here: 361 us
  waiting for transfers between devices  175 us (48%)
  matrix products  81.6 us (22%)
  local copies, waits for them, and re-layouts  58.4 us (16%)
  blocking collectives  16.2 us (4%)
  between operations  14 us (4%)
  other arithmetic  10.1 us (3%)
  starting transfers between devices  6.13 us (2%)
    all_gather x1, waiting for transfers between devices, on_device(): delta_rows = lax.all_gather(hidden_delta, 'dp', axis=0, tiled=True)  50.5 us
    all_gather x1, waiting for transfers between devices, on_device(): lax.all_gather(grad_share.astype(jnp.bfloat16), 'space', axis=0, tiled=True)  44.3 us
    psum x1, waiting for transfers between devices, on_device(): second_total = lax.psum(step_second, 'dp')  33.9 us
    dot_general x4, matrix products, per_block(): jnp.einsum('riy,rjyc->rijc', row_part, across, precision=lax.Precision.HI...  29.9 us
    convert_element_type x4, local copies, waits for them, and re-layouts, on_device(): pooled = crop_rows(whole_map, full_weight, col_weight).astype(jnp.bfloat16)  26.3 us
    psum x1, waiting for transfers between devices, on_device(): lax.psum(jnp.dot(hidden, output_weight, preferred_element_type=jnp.float3...  22.9 us
    reduce_scatter x1, waiting for transfers between devices, on_device(): lax.psum_scatter(partial_grad.astype(jnp.bfloat16), 'space', scatter_dime...  22.2 us
    dot_general x4, matrix products, per_block(): jnp.einsum('riy,rijc->rjyc', row_part, grad_block, precision=lax.Precisio...  17.9 us
  transfers between devices with their start and end apart: 6, of which 5 were waited for; matrix products, arithmetic and copies ran while one was open for 23% of the time, Pallas kernels for 0%

commit v1 on v0

--- a/solution.py
+++ b/solution.py
@@ -121,7 +121,12 @@
     )
     hidden_delta = gelu_grad(pre_hidden, hidden_back).astype(jnp.bfloat16)
     column_rows = lax.all_to_all(pooled, "dp", split_axis=1, concat_axis=0, tiled=True)
-    delta_rows = lax.all_gather(hidden_delta, "dp", axis=0, tiled=True)
+    ring = [hidden_delta]
+    for hop in range(15):
+        ring.append(lax.ppermute(ring[-1], "dp", [(dev, (dev + 1) % 16) for dev in range(16)]))
+    delta_rows = jnp.roll(
+        jnp.concatenate(ring[::-1], axis=0), (lax.axis_index("dp") + 1) * ring[0].shape[0], axis=0
+    )
     first_total = lax.dot_general(
         column_rows, delta_rows, (((0,), (0,)), ((), ())), preferred_element_type=jnp.float32
     )

time: 363 us -> 443 us (1.22)
  local copies, waits for them, and re-layouts: 58.4 us -> 99.9 us
  waiting for transfers between devices: 175 us -> 212 us
    ppermute x0 -> x15, waiting for transfers between devices: none -> 145 us  [on_device(): lax.ppermute(ring[-1], 'dp', [(dev, (dev + 1) % 16) for dev in range(16)])]
    all_gather x1 -> x0, waiting for transfers between devices: 50.5 us -> none  [on_device(): delta_rows = lax.all_gather(hidden_delta, 'dp', axis=0, tiled=True)]
    all_gather x1, waiting for transfers between devices: 44.3 us -> 0.01 us  [on_device(): lax.all_gather(grad_share.astype(jnp.bfloat16), 'space', axis=0, tiled=True)]
    unnamed x21 -> x96, local copies, waits for them, and re-layouts: 6.54 us -> 47.3 us
    psum x1, waiting for transfers between devices: 33.9 us -> 0.01 us  [on_device(): second_total = lax.psum(step_second, 'dp')]
    reduce_scatter x1, waiting for transfers between devices: 22.2 us -> 44.2 us  [on_device(): lax.psum_scatter(partial_grad.astype(jnp.bfloat16), 'space', scatter_dime...]
  transfers between devices with their start and end apart: 6 -> 20, of which waited for: 5 -> 17; matrix products, arithmetic and copies ran while one was open for 23% -> 27% of each run, Pallas kernels for 0% -> 0%
where the time goes in v1:
time: 443 us; the launch traced here: 440 us
  waiting for transfers between devices  212 us (48%)
  local copies, waits for them, and re-layouts  99.9 us (23%)
  matrix products  81.6 us (18%)
  blocking collectives  15.9 us (4%)
  between operations  14.1 us (3%)
  other arithmetic  10.1 us (2%)
  starting transfers between devices  6.63 us (1%)
    ppermute x15, waiting for transfers between devices, on_device(): lax.ppermute(ring[-1], 'dp', [(dev, (dev + 1) % 16) for dev in range(16)])  145 us
    unnamed x96, local copies, waits for them, and re-layouts  47.3 us
    reduce_scatter x1, waiting for transfers between devices, on_device(): lax.psum_scatter(partial_grad.astype(jnp.bfloat16), 'space', scatter_dime...  44.2 us
    dot_general x4, matrix products, per_block(): jnp.einsum('riy,rjyc->rijc', row_part, across, precision=lax.Precision.HI...  29.9 us
    convert_element_type x4, local copies, waits for them, and re-layouts, on_device(): pooled = crop_rows(whole_map, full_weight, col_weight).astype(jnp.bfloat16)  26.4 us
    psum x1, waiting for transfers between devices, on_device(): lax.psum(jnp.dot(hidden, output_weight, preferred_element_type=jnp.float3...  22.9 us
    dot_general x4, matrix products, per_block(): jnp.einsum('riy,rijc->rjyc', row_part, grad_block, precision=lax.Precisio...  17.9 us
    all_gather x1, blocking collectives, on_device(): whole_map = lax.all_gather(own_map, 'space', axis=0, tiled=True)  15.9 us
  transfers between devices with their start and end apart: 20, of which 17 were waited for; matrix products, arithmetic and copies ran while one was open for 27% of the time, Pallas kernels for 0%

profile of v1, /device:TPU:0, one launch (start us, length us, event | category | flops | bytes accessed | tf_op | source)
XLA Modules:
  0.0 440.4 jit_solution(5151289305594566156)
XLA Ops:
  11.3 15.9 %all-gather = bf16[1,24,84,256]{3,2,0,1:T(8,128)(2,1)S(1)} all-gather(bf16[1,12,84,256]{3,2,0,1:T(8,128)(2,1)S(1)} %bitcast.119), channel_id=2, replica_groups=mesh['dp'=16,'space'=2] {'space'}, dimensions={1}, use_global_device_ids=true | all-gather | bytes 1548288 | tf_op jit(solution)/shard_map/all_gather | solution.py:106
  27.8 34.6 %while.21 = (s32[]{:T(128)}, bf16[4,32,7,7,256]{4,2,3,1,0:T(8,128)(2,1)}, f32[4,32,7,24]{3,2,1,0:T(8,128)S(1)}, bf16[4,32,7,84]{3,1,0,2:T(8,128)(2,1)S(1)}, bf16[84,6144]{1,0:T(8,128)(2,1)S(1)}, /*index=5*/s32[]{:T(128)}) while((s32[]{:T(128)}, bf16[4,32,7,7,256]{4,2,3,1,0:T(8,128)(2,1)}, f32[4,32,7,24]{3,2,1,0:T(8,128)S(1)}, ...), condition=%wide.region_3.4_spmd, body=%wide.region_2.0_spmd.sunk | while | flops 346816512 | bytes 18293832 | solution.py:54
  29.0 7.5 %bitcast_dynamic-update-slice_fusion.2 = bf16[4,32,7,7,256]{4,2,3,1,0:T(8,128)(2,1)} fusion(bf16[4,32,7,7,256]{4,2,3,1,0:T(8,128)(2,1)} %get-tuple-element.230, s32[]{:T(128)} %get-tuple-element.229, f32[32,7,24,256]{3,0,2,1:T(8,128)S(1)} %fusion.67, f32[4,32,7,24]{3,2,1,0:T(8,128)S(1)} %get-tuple-element.237), kind=kOutput, calls=%fused_computation.2.clone.1 | convolution fusion | flops 115605504 | bytes 7472128 | tf_op jit(solution)/shard_map/while/body/eval_jaxpr/riy,rjyc->rijc/dot_general | solution.py:52
  37.6 7.5 %bitcast_dynamic-update-slice_fusion.2 = bf16[4,32,7,7,256]{4,2,3,1,0:T(8,128)(2,1)} fusion(bf16[4,32,7,7,256]{4,2,3,1,0:T(8,128)(2,1)} %get-tuple-element.230, s32[]{:T(128)} %get-tuple-element.229, f32[32,7,24,256]{3,0,2,1:T(8,128)S(1)} %fusion.67, f32[4,32,7,24]{3,2,1,0:T(8,128)S(1)} %get-tuple-element.237), kind=kOutput, calls=%fused_computation.2.clone.1 | convolution fusion | flops 115605504 | bytes 7472128 | tf_op jit(solution)/shard_map/while/body/eval_jaxpr/riy,rjyc->rijc/dot_general | solution.py:52
  46.3 7.5 %bitcast_dynamic-update-slice_fusion.2 = bf16[4,32,7,7,256]{4,2,3,1,0:T(8,128)(2,1)} fusion(bf16[4,32,7,7,256]{4,2,3,1,0:T(8,128)(2,1)} %get-tuple-element.230, s32[]{:T(128)} %get-tuple-element.229, f32[32,7,24,256]{3,0,2,1:T(8,128)S(1)} %fusion.67, f32[4,32,7,24]{3,2,1,0:T(8,128)S(1)} %get-tuple-element.237), kind=kOutput, calls=%fused_computation.2.clone.1 | convolution fusion | flops 115605504 | bytes 7472128 | tf_op jit(solution)/shard_map/while/body/eval_jaxpr/riy,rjyc->rijc/dot_general | solution.py:52
  54.9 7.5 %bitcast_dynamic-update-slice_fusion.2 = bf16[4,32,7,7,256]{4,2,3,1,0:T(8,128)(2,1)} fusion(bf16[4,32,7,7,256]{4,2,3,1,0:T(8,128)(2,1)} %get-tuple-element.230, s32[]{:T(128)} %get-tuple-element.229, f32[32,7,24,256]{3,0,2,1:T(8,128)S(1)} %fusion.67, f32[4,32,7,24]{3,2,1,0:T(8,128)S(1)} %get-tuple-element.237), kind=kOutput, calls=%fused_computation.2.clone.1 | convolution fusion | flops 115605504 | bytes 7472128 | tf_op jit(solution)/shard_map/while/body/eval_jaxpr/riy,rjyc->rijc/dot_general | solution.py:52
  62.4 5.1 %copy.77 = bf16[4,32,7,7,256]{4,3,2,1,0:T(8,128)(2,1)} copy(bf16[4,32,7,7,256]{4,2,3,1,0:T(8,128)(2,1)} %get-tuple-element.57) | data formatting | bytes 6422528 | tf_op jit(solution)/shard_map/convert_element_type | solution.py:107
  67.5 5.6 %convert_element_type.132 = bf16[128,12544]{1,0:T(8,128)(2,1)S(1)} reshape(bf16[4,32,7,7,256]{4,3,2,1,0:T(8,128)(2,1)} %copy.77) | data formatting | bytes 6422528 | tf_op jit(solution)/shard_map/convert_element_type | solution.py:107
  73.1 3.8 fusion.41
  78.7 22.9 %all-reduce.3.cloned.1.call-done = bf16[128,512]{1,0:T(8,128)(2,1)} async-done(((bf16[128,512]{1,0:T(8,128)(2,1)}), bf16[128,512]{1,0:T(8,128)(2,1)}) %all-reduce.3.cloned.1.call-update) | async-done | bytes 131088 | tf_op jit(solution)/shard_map/psum | solution.py:110
  105.3 6.8 %convolution_convert_fusion = bf16[128,12544]{1,0:T(8,128)(2,1)} fusion(bf16[128,256]{1,0:T(8,128)(2,1)S(1)} %fusion.38, bf16[12544,256]{1,0:T(8,128)(2,1)} %param.14), kind=kOutput, calls=%fused_computation.21 | convolution fusion | flops 823689216 | bytes 9699328 | tf_op jit(solution)/shard_map/dot_general | solution.py:133
  112.1 44.2 %reduce-scatter.2.cloned.1.call-done = bf16[64,12544]{1,0:T(8,128)(2,1)} async-done(((bf16[128,12544]{1,0:T(8,128)(2,1)}), bf16[64,12544]{1,0:T(8,128)(2,1)}) %reduce-scatter.2.cloned.1.call-update) | async-done | bytes 1605648 | tf_op jit(solution)/shard_map/reduce_scatter | solution.py:136
  156.4 9.3 %convert_element_type.129 = bf16[128,16,784]{2,1,0:T(8,128)(2,1)} reshape(bf16[4,32,7,7,256]{4,3,2,1,0:T(8,128)(2,1)} %copy.77) | data formatting | bytes 6422528 | tf_op jit(solution)/shard_map/convert_element_type | solution.py:107
  165.6 6.4 %copy.78 = bf16[128,16,784]{0,2,1:T(8,128)(2,1)} copy(bf16[128,16,784]{2,1,0:T(8,128)(2,1)} %convert_element_type.129) | data formatting | bytes 6422528 | tf_op jit(solution)/shard_map/convert_element_type | solution.py:107
  172.1 5.8 %all-to-all-start = ((bf16[128,16,784]{0,2,1:T(8,128)(2,1)}), bf16[128,16,784]{0,2,1:T(8,128)(2,1)S(1)}, u32[]{:S(2)}, u32[]{:S(2)}) async-start(bf16[128,16,784]{0,2,1:T(8,128)(2,1)} %copy.78), calls=%async_computation | async-start | bytes 6422528 | tf_op jit(solution)/shard_map/all_to_all | solution.py:123
  178.4 57.9 %collective-permute-done = bf16[128,256]{1,0:T(8,128)(2,1)S(1)} collective-permute-done((bf16[128,256]{1,0:T(8,128)(2,1)}, bf16[128,256]{1,0:T(8,128)(2,1)S(1)}, u32[]{:S(2)}, u32[]{:S(2)}) %collective-permute-start) | collective-permute-done | bytes 65568 | tf_op jit(solution)/shard_map/ppermute | solution.py:126
  237.0 6.5 %collective-permute-done.1 = bf16[128,256]{1,0:T(8,128)(2,1)S(1)} collective-permute-done((bf16[128,256]{1,0:T(8,128)(2,1)S(1)}, bf16[128,256]{1,0:T(8,128)(2,1)S(1)}, u32[]{:S(2)}, u32[]{:S(2)}) %collective-permute-start.1) | collective-permute-done | bytes 65568 | tf_op jit(solution)/shard_map/ppermute | solution.py:126
  244.1 6.5 %collective-permute-done.2 = bf16[128,256]{1,0:T(8,128)(2,1)S(1)} collective-permute-done((bf16[128,256]{1,0:T(8,128)(2,1)S(1)}, bf16[128,256]{1,0:T(8,128)(2,1)S(1)}, u32[]{:S(2)}, u32[]{:S(2)}) %collective-permute-start.2) | collective-permute-done | bytes 65568 | tf_op jit(solution)/shard_map/ppermute | solution.py:126
  251.2 6.4 %collective-permute-done.3 = bf16[128,256]{1,0:T(8,128)(2,1)S(1)} collective-permute-done((bf16[128,256]{1,0:T(8,128)(2,1)S(1)}, bf16[128,256]{1,0:T(8,128)(2,1)S(1)}, u32[]{:S(2)}, u32[]{:S(2)}) %collective-permute-start.3) | collective-permute-done | bytes 65568 | tf_op jit(solution)/shard_map/ppermute | solution.py:126
  258.2 6.4 %collective-permute-done.4 = bf16[128,256]{1,0:T(8,128)(2,1)S(1)} collective-permute-done((bf16[128,256]{1,0:T(8,128)(2,1)S(1)}, bf16[128,256]{1,0:T(8,128)(2,1)S(1)}, u32[]{:S(2)}, u32[]{:S(2)}) %collective-permute-start.4) | collective-permute-done | bytes 65568 | tf_op jit(solution)/shard_map/ppermute | solution.py:126
  265.2 6.4 %collective-permute-done.5 = bf16[128,256]{1,0:T(8,128)(2,1)S(1)} collective-permute-done((bf16[128,256]{1,0:T(8,128)(2,1)S(1)}, bf16[128,256]{1,0:T(8,128)(2,1)S(1)}, u32[]{:S(2)}, u32[]{:S(2)}) %collective-permute-start.5) | collective-permute-done | bytes 65568 | tf_op jit(solution)/shard_map/ppermute | solution.py:126
  272.2 6.4 %collective-permute-done.6 = bf16[128,256]{1,0:T(8,128)(2,1)S(1)} collective-permute-done((bf16[128,256]{1,0:T(8,128)(2,1)S(1)}, bf16[128,256]{1,0:T(8,128)(2,1)S(1)}, u32[]{:S(2)}, u32[]{:S(2)}) %collective-permute-start.6) | collective-permute-done | bytes 65568 | tf_op jit(solution)/shard_map/ppermute | solution.py:126
  279.3 6.4 %collective-permute-done.7 = bf16[128,256]{1,0:T(8,128)(2,1)S(1)} collective-permute-done((bf16[128,256]{1,0:T(8,128)(2,1)S(1)}, bf16[128,256]{1,0:T(8,128)(2,1)S(1)}, u32[]{:S(2)}, u32[]{:S(2)}) %collective-permute-start.7) | collective-permute-done | bytes 65568 | tf_op jit(solution)/shard_map/ppermute | solution.py:126
  286.3 6.4 %collective-permute-done.8 = bf16[128,256]{1,0:T(8,128)(2,1)S(1)} collective-permute-done((bf16[128,256]{1,0:T(8,128)(2,1)S(1)}, bf16[128,256]{1,0:T(8,128)(2,1)S(1)}, u32[]{:S(2)}, u32[]{:S(2)}) %collective-permute-start.8) | collective-permute-done | bytes 65568 | tf_op jit(solution)/shard_map/ppermute | solution.py:126
  293.3 6.5 %collective-permute-done.9 = bf16[128,256]{1,0:T(8,128)(2,1)} collective-permute-done((bf16[128,256]{1,0:T(8,128)(2,1)S(1)}, bf16[128,256]{1,0:T(8,128)(2,1)}, u32[]{:S(2)}, u32[]{:S(2)}) %collective-permute-start.9) | collective-permute-done | bytes 65568 | tf_op jit(solution)/shard_map/ppermute | solution.py:126
  299.8 6.7 %collective-permute-done.10 = bf16[128,256]{1,0:T(8,128)(2,1)} collective-permute-done((bf16[128,256]{1,0:T(8,128)(2,1)}, bf16[128,256]{1,0:T(8,128)(2,1)}, u32[]{:S(2)}, u32[]{:S(2)}) %collective-permute-start.10) | collective-permute-done | bytes 65568 | tf_op jit(solution)/shard_map/ppermute | solution.py:126
  306.5 6.6 %collective-permute-done.11 = bf16[128,256]{1,0:T(8,128)(2,1)S(1)} collective-permute-done((bf16[128,256]{1,0:T(8,128)(2,1)}, bf16[128,256]{1,0:T(8,128)(2,1)S(1)}, u32[]{:S(2)}, u32[]{:S(2)}) %collective-permute-start.11) | collective-permute-done | bytes 65568 | tf_op jit(solution)/shard_map/ppermute | solution.py:126
  313.9 6.3 %collective-permute-done.12 = bf16[128,256]{1,0:T(8,128)(2,1)} collective-permute-done((bf16[128,256]{1,0:T(8,128)(2,1)S(1)}, bf16[128,256]{1,0:T(8,128)(2,1)}, u32[]{:S(2)}, u32[]{:S(2)}) %collective-permute-start.12) | collective-permute-done | bytes 65568 | tf_op jit(solution)/shard_map/ppermute | solution.py:126
  322.2 4.7 %collective-permute-done.13 = bf16[128,256]{1,0:T(8,128)(2,1)} collective-permute-done((bf16[128,256]{1,0:T(8,128)(2,1)}, bf16[128,256]{1,0:T(8,128)(2,1)}, u32[]{:S(2)}, u32[]{:S(2)}) %collective-permute-start.13) | collective-permute-done | bytes 65568 | tf_op jit(solution)/shard_map/ppermute | solution.py:126
  326.9 2.0 fusion.40
  329.0 4.6 %collective-permute-done.14 = bf16[128,256]{1,0:T(8,128)(2,1)} collective-permute-done((bf16[128,256]{1,0:T(8,128)(2,1)}, bf16[128,256]{1,0:T(8,128)(2,1)}, u32[]{:S(2)}, u32[]{:S(2)}) %collective-permute-start.14) | collective-permute-done | bytes 65568 | tf_op jit(solution)/shard_map/ppermute | solution.py:126
  368.2 3.1 fusion.18
  371.3 5.1 %convert.3 = f32[4,32,12544]{2,1,0:T(8,128)} convert(bf16[4,32,12544]{2,1,0:T(8,128)(2,1)} %bitcast.114) | non-fusion elementwise | flops 1605632 | bytes 9633792 | tf_op jit(solution)/shard_map/reshape | solution.py:86
  376.4 51.9 %while.22 = (s32[]{:T(128)}, f32[84,3072]{1,0:T(8,128)}, bf16[4,32,7,84]{3,2,1,0:T(8,128)(2,1)}, f32[4,32,12544]{2,1,0:T(8,128)}, f32[4,32,7,12]{3,2,1,0:T(8,128)}, /*index=5*/s32[]{:T(128)}, s32[]{:T(128)}) while((s32[]{:T(128)}, f32[84,3072]{1,0:T(8,128)}, bf16[4,32,7,84]{3,2,1,0:T(8,128)(2,1)}, f32[4,32,12544]{2,1,0:T(8,128)}, ...), condition=%wide.region_9.10_spmd.clone, body=%wide.region_8.9_spmd.clone.sunk | while | flops 751951872 | bytes 21422432 | solution.py:88
  378.4 4.5 %fusion.72 = f32[32,7,256,12]{2,3,1,0:T(8,128)S(1)} fusion(f32[32,7,7,256]{3,2,1,0:T(8,128)S(1)} %reshape.239, f32[4,32,7,12]{3,2,1,0:T(8,128)} %get-tuple-element.259, s32[]{:T(128)} %get-tuple-element.248), kind=kOutput, calls=%fused_computation.14.clone.1 | convolution fusion | flops 57802752 | bytes 4489728 | tf_op jit(solution)/shard_map/while/body/eval_jaxpr/riy,rijc->rjyc/dot_general | solution.py:72
  382.9 2.4 copy.120
  386.2 2.2 convolution_add_fusion.2
  390.5 4.5 %fusion.72 = f32[32,7,256,12]{2,3,1,0:T(8,128)S(1)} fusion(f32[32,7,7,256]{3,2,1,0:T(8,128)S(1)} %reshape.239, f32[4,32,7,12]{3,2,1,0:T(8,128)} %get-tuple-element.259, s32[]{:T(128)} %get-tuple-element.248), kind=kOutput, calls=%fused_computation.14.clone.1 | convolution fusion | flops 57802752 | bytes 4489728 | tf_op jit(solution)/shard_map/while/body/eval_jaxpr/riy,rijc->rjyc/dot_general | solution.py:72
  394.9 2.4 copy.120
  398.3 3.5 convolution_add_fusion.2
  403.8 4.5 %fusion.72 = f32[32,7,256,12]{2,3,1,0:T(8,128)S(1)} fusion(f32[32,7,7,256]{3,2,1,0:T(8,128)S(1)} %reshape.239, f32[4,32,7,12]{3,2,1,0:T(8,128)} %get-tuple-element.259, s32[]{:T(128)} %get-tuple-element.248), kind=kOutput, calls=%fused_computation.14.clone.1 | convolution fusion | flops 57802752 | bytes 4489728 | tf_op jit(solution)/shard_map/while/body/eval_jaxpr/riy,rijc->rjyc/dot_general | solution.py:72
  408.2 2.4 copy.120
  411.6 3.5 convolution_add_fusion.2
  417.1 4.5 %fusion.72 = f32[32,7,256,12]{2,3,1,0:T(8,128)S(1)} fusion(f32[32,7,7,256]{3,2,1,0:T(8,128)S(1)} %reshape.239, f32[4,32,7,12]{3,2,1,0:T(8,128)} %get-tuple-element.259, s32[]{:T(128)} %get-tuple-element.248), kind=kOutput, calls=%fused_computation.14.clone.1 | convolution fusion | flops 57802752 | bytes 4489728 | tf_op jit(solution)/shard_map/while/body/eval_jaxpr/riy,rijc->rjyc/dot_general | solution.py:72
  421.5 2.4 copy.120
  424.9 3.5 convolution_add_fusion.2
  430.0 2.0 copy.84
  432.0 1.9 copy.167
  (173 shorter events, 71.2 us)
Async XLA Ops:
  7.2 70.5 %copy-start = (bf16[256,512]{1,0:T(8,128)(2,1)S(1)}, bf16[256,512]{1,0:T(8,128)(2,1)}, u32[]{:S(2)}) copy-start(bf16[256,512]{1,0:T(8,128)(2,1)} %param.15) | copy-start | bytes 786436
  7.2 4.1 copy-start.8
  7.2 94.5 %all-reduce.3.cloned.1.call-start = ((), (), s32[]{:S(2)}) async-start(), calls=%async_computation.2 | async-start | bytes 262144 | tf_op jit(solution)/shard_map/psum | solution.py:110
  10.7 16.7 %copy-start.2 = (bf16[128,7,84]{0,2,1:T(8,128)(2,1)}, bf16[128,7,84]{0,2,1:T(8,128)(2,1)S(1)}, u32[]{:S(2)}) copy-start(bf16[128,7,84]{0,2,1:T(8,128)(2,1)S(1)} %multiply_convert_fusion) | copy-start | bytes 451588
  77.0 0.7 copy-start.4
  78.5 77.9 %reduce-scatter.2.cloned.1.call-start = ((), (), s32[]{:S(2)}) async-start(), calls=%async_computation.4 | async-start | bytes 4816896 | tf_op jit(solution)/shard_map/reduce_scatter | solution.py:136
  102.8 0.7 copy-start.9
  104.6 0.6 copy-start.6
  112.1 259.2 %all-gather.3.cloned.1.call-start = ((), (), s32[]{:S(2)}) async-start(), calls=%async_computation.5 | async-start | bytes 4816896 | tf_op jit(solution)/shard_map/all_gather | solution.py:139
  172.1 148.2 %copy-start.3 = (bf16[128,7,84]{0,2,1:T(8,128)(2,1)S(1)}, bf16[128,7,84]{0,2,1:T(8,128)(2,1)}, u32[]{:S(2)}) copy-start(bf16[128,7,84]{0,2,1:T(8,128)(2,1)} %copy-done.2) | copy-start | bytes 451588
  172.1 154.8 %copy-start.5 = (f32[128,256]{1,0:T(8,128)S(1)}, f32[128,256]{1,0:T(8,128)}, u32[]{:S(2)}) copy-start(f32[128,256]{1,0:T(8,128)} %copy-done.4) | copy-start | bytes 393220
  172.1 196.1 %all-to-all-start = ((bf16[128,16,784]{0,2,1:T(8,128)(2,1)}), bf16[128,16,784]{0,2,1:T(8,128)(2,1)S(1)}, u32[]{:S(2)}, u32[]{:S(2)}) async-start(bf16[128,16,784]{0,2,1:T(8,128)(2,1)} %copy.78), calls=%async_computation | async-start | bytes 6422528 | tf_op jit(solution)/shard_map/all_to_all | solution.py:123
  177.9 254.1 %all-reduce.5.cloned.1.call-start = ((), (), s32[]{:S(2)}) async-start(), calls=%async_computation.3 | async-start | bytes 1048576 | tf_op jit(solution)/shard_map/psum | solution.py:118
  177.9 58.4 %collective-permute-start = (bf16[128,256]{1,0:T(8,128)(2,1)}, bf16[128,256]{1,0:T(8,128)(2,1)S(1)}, u32[]{:S(2)}, u32[]{:S(2)}) collective-permute-start(bf16[128,256]{1,0:T(8,128)(2,1)} %copy-done.6), channel_id=1, source_target_pairs={{0,2},{2,4},{4,6},{6,8},{8,10},{10,12},{12,14},{14,16},{16,18},{18... | collective-permute-start | bytes 196616 | tf_op jit(solution)/shard_map/ppermute | solution.py:126
  236.3 0.6 copy-start.10
  237.0 6.5 %collective-permute-start.1 = (bf16[128,256]{1,0:T(8,128)(2,1)S(1)}, bf16[128,256]{1,0:T(8,128)(2,1)S(1)}, u32[]{:S(2)}, u32[]{:S(2)}) collective-permute-start(bf16[128,256]{1,0:T(8,128)(2,1)S(1)} %collective-permute-done), channel_id=1, source_target_pairs={{0,2},{2,4},{4,6},{6,8},{8,10},{10,12},{12,14},{14,16},{16,18},{18... | collective-permute-start | bytes 196616 | tf_op jit(solution)/shard_map/ppermute | solution.py:126
  243.4 0.6 copy-start.12
  244.1 6.5 %collective-permute-start.2 = (bf16[128,256]{1,0:T(8,128)(2,1)S(1)}, bf16[128,256]{1,0:T(8,128)(2,1)S(1)}, u32[]{:S(2)}, u32[]{:S(2)}) collective-permute-start(bf16[128,256]{1,0:T(8,128)(2,1)S(1)} %collective-permute-done.1), channel_id=1, source_target_pairs={{0,2},{2,4},{4,6},{6,8},{8,10},{10,12},{12,14},{14,16},{16,18},{18... | collective-permute-start | bytes 196616 | tf_op jit(solution)/shard_map/ppermute | solution.py:126
  251.2 6.4 %collective-permute-start.3 = (bf16[128,256]{1,0:T(8,128)(2,1)S(1)}, bf16[128,256]{1,0:T(8,128)(2,1)S(1)}, u32[]{:S(2)}, u32[]{:S(2)}) collective-permute-start(bf16[128,256]{1,0:T(8,128)(2,1)S(1)} %collective-permute-done.2), channel_id=1, source_target_pairs={{0,2},{2,4},{4,6},{6,8},{8,10},{10,12},{12,14},{14,16},{16,18},{18... | collective-permute-start | bytes 196616 | tf_op jit(solution)/shard_map/ppermute | solution.py:126
  257.6 0.6 copy-start.16
  258.2 6.4 %collective-permute-start.4 = (bf16[128,256]{1,0:T(8,128)(2,1)S(1)}, bf16[128,256]{1,0:T(8,128)(2,1)S(1)}, u32[]{:S(2)}, u32[]{:S(2)}) collective-permute-start(bf16[128,256]{1,0:T(8,128)(2,1)S(1)} %collective-permute-done.3), channel_id=1, source_target_pairs={{0,2},{2,4},{4,6},{6,8},{8,10},{10,12},{12,14},{14,16},{16,18},{18... | collective-permute-start | bytes 196616 | tf_op jit(solution)/shard_map/ppermute | solution.py:126
  264.6 0.6 copy-start.18
  265.2 6.4 %collective-permute-start.5 = (bf16[128,256]{1,0:T(8,128)(2,1)S(1)}, bf16[128,256]{1,0:T(8,128)(2,1)S(1)}, u32[]{:S(2)}, u32[]{:S(2)}) collective-permute-start(bf16[128,256]{1,0:T(8,128)(2,1)S(1)} %collective-permute-done.4), channel_id=1, source_target_pairs={{0,2},{2,4},{4,6},{6,8},{8,10},{10,12},{12,14},{14,16},{16,18},{18... | collective-permute-start | bytes 196616 | tf_op jit(solution)/shard_map/ppermute | solution.py:126
  271.6 0.6 copy-start.20
  272.2 6.4 %collective-permute-start.6 = (bf16[128,256]{1,0:T(8,128)(2,1)S(1)}, bf16[128,256]{1,0:T(8,128)(2,1)S(1)}, u32[]{:S(2)}, u32[]{:S(2)}) collective-permute-start(bf16[128,256]{1,0:T(8,128)(2,1)S(1)} %collective-permute-done.5), channel_id=1, source_target_pairs={{0,2},{2,4},{4,6},{6,8},{8,10},{10,12},{12,14},{14,16},{16,18},{18... | collective-permute-start | bytes 196616 | tf_op jit(solution)/shard_map/ppermute | solution.py:126
  279.2 6.4 %collective-permute-start.7 = (bf16[128,256]{1,0:T(8,128)(2,1)S(1)}, bf16[128,256]{1,0:T(8,128)(2,1)S(1)}, u32[]{:S(2)}, u32[]{:S(2)}) collective-permute-start(bf16[128,256]{1,0:T(8,128)(2,1)S(1)} %collective-permute-done.6), channel_id=1, source_target_pairs={{0,2},{2,4},{4,6},{6,8},{8,10},{10,12},{12,14},{14,16},{16,18},{18... | collective-permute-start | bytes 196616 | tf_op jit(solution)/shard_map/ppermute | solution.py:126
  285.6 0.6 copy-start.24
  286.3 6.4 %collective-permute-start.8 = (bf16[128,256]{1,0:T(8,128)(2,1)S(1)}, bf16[128,256]{1,0:T(8,128)(2,1)S(1)}, u32[]{:S(2)}, u32[]{:S(2)}) collective-permute-start(bf16[128,256]{1,0:T(8,128)(2,1)S(1)} %collective-permute-done.7), channel_id=1, source_target_pairs={{0,2},{2,4},{4,6},{6,8},{8,10},{10,12},{12,14},{14,16},{16,18},{18... | collective-permute-start | bytes 196616 | tf_op jit(solution)/shard_map/ppermute | solution.py:126
  292.7 0.6 copy-start.26
  293.3 6.5 %collective-permute-start.9 = (bf16[128,256]{1,0:T(8,128)(2,1)S(1)}, bf16[128,256]{1,0:T(8,128)(2,1)}, u32[]{:S(2)}, u32[]{:S(2)}) collective-permute-start(bf16[128,256]{1,0:T(8,128)(2,1)S(1)} %collective-permute-done.8), channel_id=1, source_target_pairs={{0,2},{2,4},{4,6},{6,8},{8,10},{10,12},{12,14},{14,16},{16,18},{18... | collective-permute-start | bytes 196616 | tf_op jit(solution)/shard_map/ppermute | solution.py:126
  299.8 6.7 %collective-permute-start.10 = (bf16[128,256]{1,0:T(8,128)(2,1)}, bf16[128,256]{1,0:T(8,128)(2,1)}, u32[]{:S(2)}, u32[]{:S(2)}) collective-permute-start(bf16[128,256]{1,0:T(8,128)(2,1)} %collective-permute-done.9), channel_id=1, source_target_pairs={{0,2},{2,4},{4,6},{6,8},{8,10},{10,12},{12,14},{14,16},{16,18},{18... | collective-permute-start | bytes 196616 | tf_op jit(solution)/shard_map/ppermute | solution.py:126
  306.5 6.6 %collective-permute-start.11 = (bf16[128,256]{1,0:T(8,128)(2,1)}, bf16[128,256]{1,0:T(8,128)(2,1)S(1)}, u32[]{:S(2)}, u32[]{:S(2)}) collective-permute-start(bf16[128,256]{1,0:T(8,128)(2,1)} %collective-permute-done.10), channel_id=1, source_target_pairs={{0,2},{2,4},{4,6},{6,8},{8,10},{10,12},{12,14},{14,16},{16,18},{18... | collective-permute-start | bytes 196616 | tf_op jit(solution)/shard_map/ppermute | solution.py:126
  313.1 0.6 copy-start.28
  313.7 6.5 %collective-permute-start.12 = (bf16[128,256]{1,0:T(8,128)(2,1)S(1)}, bf16[128,256]{1,0:T(8,128)(2,1)}, u32[]{:S(2)}, u32[]{:S(2)}) collective-permute-start(bf16[128,256]{1,0:T(8,128)(2,1)S(1)} %collective-permute-done.11), channel_id=1, source_target_pairs={{0,2},{2,4},{4,6},{6,8},{8,10},{10,12},{12,14},{14,16},{16,18},{18... | collective-permute-start | bytes 196616 | tf_op jit(solution)/shard_map/ppermute | solution.py:126
  320.2 6.7 %collective-permute-start.13 = (bf16[128,256]{1,0:T(8,128)(2,1)}, bf16[128,256]{1,0:T(8,128)(2,1)}, u32[]{:S(2)}, u32[]{:S(2)}) collective-permute-start(bf16[128,256]{1,0:T(8,128)(2,1)} %collective-permute-done.12), channel_id=1, source_target_pairs={{0,2},{2,4},{4,6},{6,8},{8,10},{10,12},{12,14},{14,16},{16,18},{18... | collective-permute-start | bytes 196616 | tf_op jit(solution)/shard_map/ppermute | solution.py:126
  321.1 31.4 %copy-start.11 = (bf16[128,256]{1,0:T(8,128)(2,1)S(1)}, bf16[128,256]{1,0:T(8,128)(2,1)}, u32[]{:S(2)}) copy-start(bf16[128,256]{1,0:T(8,128)(2,1)} %copy-done.10) | copy-start | bytes 196612
  321.1 32.0 %copy-start.7 = (bf16[128,256]{1,0:T(8,128)(2,1)S(1)}, bf16[128,256]{1,0:T(8,128)(2,1)}, u32[]{:S(2)}) copy-start(bf16[128,256]{1,0:T(8,128)(2,1)} %copy-done.6) | copy-start | bytes 196612
  326.9 6.7 %collective-permute-start.14 = (bf16[128,256]{1,0:T(8,128)(2,1)}, bf16[128,256]{1,0:T(8,128)(2,1)}, u32[]{:S(2)}, u32[]{:S(2)}) collective-permute-start(bf16[128,256]{1,0:T(8,128)(2,1)} %collective-permute-done.13), channel_id=1, source_target_pairs={{0,2},{2,4},{4,6},{6,8},{8,10},{10,12},{12,14},{14,16},{16,18},{18... | collective-permute-start | bytes 196616 | tf_op jit(solution)/shard_map/ppermute | solution.py:126
  328.9 22.4 %copy-start.15 = (bf16[128,256]{1,0:T(8,128)(2,1)S(1)}, bf16[128,256]{1,0:T(8,128)(2,1)}, u32[]{:S(2)}) copy-start(bf16[128,256]{1,0:T(8,128)(2,1)} %copy-done.14) | copy-start | bytes 196612
  328.9 23.0 %copy-start.13 = (bf16[128,256]{1,0:T(8,128)(2,1)S(1)}, bf16[128,256]{1,0:T(8,128)(2,1)}, u32[]{:S(2)}) copy-start(bf16[128,256]{1,0:T(8,128)(2,1)} %copy-done.12) | copy-start | bytes 196612
  328.9 36.1 %copy-start.17 = (bf16[128,256]{1,0:T(8,128)(2,1)S(1)}, bf16[128,256]{1,0:T(8,128)(2,1)}, u32[]{:S(2)}) copy-start(bf16[128,256]{1,0:T(8,128)(2,1)} %copy-done.16) | copy-start | bytes 196612
  328.9 29.3 %copy-start.29 = (bf16[128,256]{1,0:T(8,128)(2,1)S(1)}, bf16[128,256]{1,0:T(8,128)(2,1)}, u32[]{:S(2)}) copy-start(bf16[128,256]{1,0:T(8,128)(2,1)} %copy-done.28) | copy-start | bytes 196612
  328.9 32.9 %copy-start.27 = (bf16[128,256]{1,0:T(8,128)(2,1)S(1)}, bf16[128,256]{1,0:T(8,128)(2,1)}, u32[]{:S(2)}) copy-start(bf16[128,256]{1,0:T(8,128)(2,1)} %copy-done.26) | copy-start | bytes 196612
  328.9 33.5 %copy-start.25 = (bf16[128,256]{1,0:T(8,128)(2,1)S(1)}, bf16[128,256]{1,0:T(8,128)(2,1)}, u32[]{:S(2)}) copy-start(bf16[128,256]{1,0:T(8,128)(2,1)} %copy-done.24) | copy-start | bytes 196612
  328.9 34.1 %copy-start.23 = (bf16[128,256]{1,0:T(8,128)(2,1)S(1)}, bf16[128,256]{1,0:T(8,128)(2,1)}, u32[]{:S(2)}) copy-start(bf16[128,256]{1,0:T(8,128)(2,1)} %copy-done.22) | copy-start | bytes 196612
  329.0 34.7 %copy-start.21 = (bf16[128,256]{1,0:T(8,128)(2,1)S(1)}, bf16[128,256]{1,0:T(8,128)(2,1)}, u32[]{:S(2)}) copy-start(bf16[128,256]{1,0:T(8,128)(2,1)} %copy-done.20) | copy-start | bytes 196612
  329.0 35.4 %copy-start.19 = (bf16[128,256]{1,0:T(8,128)(2,1)S(1)}, bf16[128,256]{1,0:T(8,128)(2,1)}, u32[]{:S(2)}) copy-start(bf16[128,256]{1,0:T(8,128)(2,1)} %copy-done.18) | copy-start | bytes 196612
  428.4 5.5 %copy-start.1 = (bf16[256,512]{1,0:T(8,128)(2,1)S(1)}, bf16[256,512]{1,0:T(8,128)(2,1)}, u32[]{:S(2)}) copy-start(bf16[256,512]{1,0:T(8,128)(2,1)} %param.15) | copy-start | bytes 786436
  (2 other events, 1.2 us)
Sparse Core Ops, SparseCore 0:
  78.6 23.0 all-reduce.2
  112.2 44.1 reduce-scatter.1
  157.9 45.6 all-gather.2
  329.0 90.9 all-reduce.4
